TPU v7x, 32 devices: a whole 2x2x4 slice. The times are simulated.
32 devices in a mesh: groups: 2 (over x), steps: 16 (over z, y, core).
Axes of the slice: x: 2, y: 2, z: 4, core: 2. Of those that a mesh axis runs over, the one named last changes fastest.
Arguments:
- states: float32 [32, 4, 4096], P(('groups', 'steps')), parts along dimension 0, may hold values from -6 to 6
- t_sched: int32 [66], P('groups'), parts along dimension 0, may hold values from 0 to 999, as said below
- advances: int32 [4], P('groups'), parts along dimension 0, may hold values from 1 to 16, as said below
- in_weight: bfloat16 [320, 4], replicated, may hold values from -3 to 3
- time_weight: float32 [320, 320], replicated, may hold values from -0.3125 to 0.3125
- mid_weight: bfloat16 [320, 320], replicated, may hold values from -0.3125 to 0.3125
- out_weight: bfloat16 [4, 320], replicated, may hold values from -0.3125 to 0.3125
Outputs:
- final_states: float32 [32, 4, 4096], P(('groups', 'steps')), parts along dimension 0
- errors: float32 [4, 4, 16], P('groups', None, 'steps'), parts along dimension 0
There are 2 independent parts, one for each index of `groups`. A program takes and returns all parts, laid end to end along the dimension named above; an argument that names none is the same for every part. Nothing has to cross between parts.
Inputs may be any that keep to these rules, and one draw needn't show every extreme that they name: `t_sched`: strictly decreasing. Some round advances by exactly 16.
All inputs are finite; a program needn't handle non-finite values.
Results may differ from a plain program's by a relative error of at most 0.0024.
Values sent between devices are 32-bit elements; how exact they have to be, the bound alone decides.
A program may use at most 64 MiB of HBM per device.

v0:
```python
import functools
import math

import jax
import jax.numpy as jnp
import numpy as np
from jax import lax
from jax.experimental import pallas as pl
from jax.experimental.pallas import tpu as pltpu
from jax.sharding import PartitionSpec as P

TSTEPS = 1000
ITERS = 4
ROUNDS = 2
LANES = 128
BASE = 32
XROWS = 16
GROUP_MOST = 15


def alpha_table():
    levels = np.arange(TSTEPS, dtype=np.float64)
    low = math.sqrt(0.00085)
    high = math.sqrt(0.012)
    betas = (low + (high - low) * levels / (TSTEPS - 1)) ** 2
    return np.exp(np.cumsum(np.log1p(-betas))).astype(np.float32)


def trig_tables(width):
    half = width // 2
    freqs = np.exp(-math.log(10000.0) * np.arange(half, dtype=np.float64) / half)[:, None]
    digits = np.arange(BASE, dtype=np.float64)[None]
    high, low = freqs * digits * BASE, freqs * digits
    coarse = np.concatenate([np.cos(high), np.sin(high)]).astype(np.float32)
    fine = np.concatenate([np.cos(low), np.sin(low)]).astype(np.float32)
    return np.concatenate([coarse, fine])


def round_up(value, unit):
    return -(-value // unit) * unit


def kernel(
    n, pix, width, depth, direct,
    states_hbm, sched_ref, adv_ref, alpha_ref, inw_hbm, outw_hbm, timew_hbm, midw_hbm, trig_hbm,
    out_ref, err_ref,
    states_ref, inw_ref, outw_ref, timew, midw, trig, xin, xs, fin, errs, elines, erecv, lhs, mid, outw, inw, coef_one, coef_two,
    local, in_send, in_recv, out_send, out_recv, err_send, err_recv,
):
    lat = outw_ref.shape[0]
    ch = midw.shape[0]
    me = lax.axis_index("steps")
    span = ROUNDS * n
    f32, bf16 = jnp.float32, jnp.bfloat16

    def peer(hop):
        return lax.rem(me + hop, n)

    def source(d):
        if direct:
            return states_ref.at[0, :, pl.ds(pl.multiple_of(d * pix, LANES), pix)]
        return states_ref.at[d]

    def target(d):
        if direct:
            return out_ref.at[0, :, pl.ds(pl.multiple_of(d * pix, LANES), pix)]
        return out_ref.at[d]

    def in_copy(d, slot):
        return pltpu.make_async_remote_copy(
            src_ref=source(d), dst_ref=xin.at[slot], send_sem=in_send.at[d], recv_sem=in_recv.at[slot],
            device_id={"steps": d}, device_id_type=pl.DeviceIdType.MESH)

    def out_copy(d, slot):
        return pltpu.make_async_remote_copy(
            src_ref=fin.at[d], dst_ref=target(slot), send_sem=out_send.at[d], recv_sem=out_recv.at[slot],
            device_id={"steps": d}, device_id_type=pl.DeviceIdType.MESH)

    def err_copy(d, slot):
        return pltpu.make_async_remote_copy(
            src_ref=elines.at[d], dst_ref=erecv.at[slot], send_sem=err_send.at[d], recv_sem=err_recv.at[slot],
            device_id={"steps": d}, device_id_type=pl.DeviceIdType.MESH)

    def each_peer(act):
        if n <= 16:
            for hop in range(1, n):
                act(peer(hop))
        else:
            @pl.loop(1, n)
            def _(hop):
                act(peer(hop))

    loads = [
        pltpu.make_async_copy(source_ref, held, local.at[j])
        for j, (source_ref, held) in enumerate((
            (states_hbm, states_ref), (trig_hbm, trig), (timew_hbm, timew), (midw_hbm, midw),
            (inw_hbm, inw_ref), (outw_hbm, outw_ref)))
    ]
    for load in loads:
        load.start()
    barrier = pltpu.get_barrier_semaphore()
    each_peer(lambda d: pl.semaphore_signal(
        barrier, inc=1, device_id={"steps": d}, device_id_type=pl.DeviceIdType.MESH))

    lane = lax.broadcasted_iota(jnp.int32, (1, depth), 1) - XROWS
    member = jnp.where((lane >= 0) & (lane < 3 * span), lax.rem(jnp.maximum(lane, 0), span), -1)
    advance_one = adv_ref[0]

    def coefficients(m, stamps):
        place = jnp.where(m >= n, advance_one + m - n, m)
        now, after = sched_ref[place], sched_ref[place + 1]
        a_now = jnp.full((8, LANES), alpha_ref[now], f32)
        a_after = jnp.full((8, LANES), alpha_ref[after], f32)
        one = jnp.sqrt(a_after / a_now)
        two = jnp.sqrt(1.0 - a_after) - one * jnp.sqrt(1.0 - a_now)
        coef_one[m] = one - 1.0
        coef_two[m] = two
        return jnp.where(member == m, now, stamps)

    stamps = lax.fori_loop(0, span, coefficients, jnp.zeros((1, depth), jnp.int32), unroll=4)

    loads[0].wait()
    pl.semaphore_wait(barrier, n - 1)
    each_peer(lambda d: in_copy(d, me).start())

    digit = lax.broadcasted_iota(jnp.int32, (BASE, depth), 0)
    hot_high = (digit == lax.shift_right_logical(stamps, 5)).astype(f32)
    hot_low = (digit == lax.bitwise_and(stamps, BASE - 1)).astype(f32)
    exact = lax.Precision.HIGHEST
    for load in loads[1:]:
        load.wait()
    high = jnp.dot(trig[0:ch], hot_high, precision=exact, preferred_element_type=f32)
    low = jnp.dot(trig[ch:], hot_low, precision=exact, preferred_element_type=f32)
    half = ch // 2
    cos_h, sin_h, cos_l, sin_l = high[:half], high[half:], low[:half], low[half:]
    feats = jnp.concatenate([cos_h * cos_l - sin_h * sin_l, sin_h * cos_l + cos_h * sin_l], axis=0)
    embed = 0.5 * jnp.dot(timew[...], feats, precision=exact, preferred_element_type=f32)
    inw[...] = jnp.zeros_like(inw)
    inw[0:lat, :] = inw_ref[...].astype(f32) * 0.5
    unit = (lax.broadcasted_iota(jnp.int32, (8, depth), 0) == lane + XROWS).astype(f32)
    spread = lax.dot_general(
        inw[...], unit, (((0,), (0,)), ((), ())), precision=exact, preferred_element_type=f32)
    top = embed.astype(bf16).astype(f32)
    rest = embed - top
    middle = rest.astype(bf16).astype(f32)
    bottom = (rest - middle).astype(bf16).astype(f32)
    part = jnp.where(lane < span, top, jnp.where(lane < 2 * span, middle, bottom))
    part = jnp.where(member >= 0, part, 0.0)
    left = spread + part
    lhs[0:ch, :] = left.astype(bf16)
    mid[...] = (midw[...].astype(f32) * 0.5).astype(bf16)
    outw[...] = jnp.zeros_like(outw)
    outw[0:lat, :] = outw_ref[...].astype(f32)
    linear = 2.0 * jnp.dot(outw[...], left, precision=exact, preferred_element_type=f32)
    linear_top = linear.astype(bf16).astype(f32)
    linear_rest = linear - linear_top
    linear_middle = linear_rest.astype(bf16).astype(f32)
    linear_bottom = linear_rest - linear_middle
    lhs[ch:ch + 32, :] = jnp.concatenate(
        [linear_top, linear_middle, linear_bottom, jnp.zeros_like(linear)], axis=0).astype(bf16)

    xs[...] = jnp.zeros_like(xs)
    errs[...] = jnp.zeros_like(errs)
    if direct:
        xs[me, 0:lat, :] = states_ref[0, :, pl.ds(pl.multiple_of(me * pix, LANES), pix)]
    else:
        xs[me, 0:lat, :] = states_ref[me]

    def arrived(d):
        in_copy(d, d).wait_recv()
        xs[d, 0:lat, :] = xin[d]

    each_peer(arrived)

    hot_row = lax.broadcasted_iota(jnp.int32, (depth - XROWS, LANES), 0)
    hot_member = jnp.where(hot_row < 3 * span, lax.rem(hot_row, span), -1)
    outs = outw[...].astype(bf16)
    wide = lambda tile: jnp.concatenate([tile] * (width // LANES), axis=1) if width > LANES else tile

    def first(x, m):
        hot = wide((hot_member == m).astype(f32).astype(bf16))
        padded = jnp.concatenate([x, jnp.zeros((XROWS - 8, width), f32)], axis=0).astype(bf16)
        both = jnp.dot(lhs[...], jnp.concatenate([padded, hot], axis=0), preferred_element_type=f32)
        pre = both[0:ch]
        tail = both[ch:ch + 8] + both[ch + 8:ch + 16] + both[ch + 16:ch + 24]
        return tail, (pre + pre * jnp.tanh(pre)).astype(bf16)

    def second(tail, hidden):
        mixed = jnp.dot(mid[...], hidden, preferred_element_type=f32)
        return tail, (mixed + mixed * jnp.tanh(mixed)).astype(bf16)

    def third(tail, hidden):
        return tail + jnp.dot(outs, hidden, preferred_element_type=f32)

    def note_error(row, k, change):
        square = change * change
        if pix < width:
            square = jnp.where(lax.broadcasted_iota(jnp.int32, square.shape, 1) < pix, square, 0.0)
        total = square[:, 0:LANES]
        for start in range(LANES, width, LANES):
            total = total + square[:, start:start + LANES]
        errs[k, pl.ds(row, 1), :] = jnp.sum(total, axis=0, keepdims=True)

    def one_round(r, carry):
        def some(row, ks, running):
            count = len(ks)
            olds = [xs[k] for k in ks]
            ones = [None] * count
            twos = [None] * count
            noises = [None] * count
            for step in range(count + 2):
                if step < count:
                    ones[step] = first(olds[step], r * n + ks[step])
                if 0 <= step - 1 < count:
                    twos[step - 1] = second(*ones[step - 1])
                if 0 <= step - 2 < count:
                    noises[step - 2] = third(*twos[step - 2])
            for j, k in enumerate(ks):
                m = r * n + k
                note_error(row, k, running - olds[j])
                xs[k] = running
                running = running + (wide(coef_one[m]) * olds[j] + wide(coef_two[m]) * noises[j])
            return running

        for i in range(ITERS):
            row = r * ITERS + i
            if n <= GROUP_MOST + 1:
                running = some(row, list(range(i, n - 1)), xs[i])
            else:
                running = lax.fori_loop(i, n - 1, lambda k, held: some(row, [k], held), xs[i])
            note_error(row, n - 1, running - xs[n - 1])
            xs[n - 1] = running
        advance = adv_ref[r]

        def shift(k, carry):
            xs[k] = xs[jnp.minimum(k + advance, n - 1)]
            return carry

        lax.fori_loop(0, n, shift, 0, unroll=4)
        return carry

    lax.fori_loop(0, ROUNDS, one_round, 0)
    for k in range(n):
        fin[k] = xs[k, 0:lat, :]
    each_peer(lambda d: out_copy(d, me).start())
    cells = (ROUNDS * ITERS, LANES)
    diagonal = lax.broadcasted_iota(jnp.int32, cells, 0) == lax.broadcasted_iota(jnp.int32, cells, 1)
    for k in range(n):
        total = jnp.sum(errs[k], axis=1, keepdims=True)
        elines[k] = jnp.sum(jnp.where(diagonal, total, 0.0), axis=0, keepdims=True)
    each_peer(lambda d: err_copy(d, me).start())
    if direct:
        out_ref[0, :, pl.ds(pl.multiple_of(me * pix, LANES), pix)] = fin[me]
    else:
        out_ref[me] = fin[me]
    erecv[me] = elines[me]
    each_peer(lambda d: err_copy(d, d).wait_recv())
    sums = lax.fori_loop(0, n, lambda k, total: total + erecv[k], jnp.zeros((1, LANES), f32), unroll=4)
    means = jnp.sum(jnp.where(diagonal, sums, 0.0), axis=1, keepdims=True) * (1.0 / (lat * n * pix))
    for r in range(ROUNDS):
        err_ref[r] = means[r * ITERS:(r + 1) * ITERS]
    each_peer(lambda d: out_copy(d, d).wait_recv())
    each_peer(lambda d: in_copy(d, me).wait_send())
    each_peer(lambda d: out_copy(d, me).wait_send())
    each_peer(lambda d: err_copy(d, me).wait_send())


def shards(states, t_sched, advances, in_weight, time_weight, mid_weight, out_weight):
    n = lax.axis_size("steps")
    _, lat, rows = states.shape
    ch = mid_weight.shape[0]
    pix = rows // n
    direct = pix % LANES == 0
    width = round_up(pix, LANES)
    depth = round_up(XROWS + 3 * ROUNDS * n, LANES)
    if direct:
        sent = states
        out_shape = states.shape
    else:
        sent = jnp.pad(states.reshape(lat, n, pix).transpose(1, 0, 2), ((0, 0), (0, 0), (0, width - pix)))
        out_shape = sent.shape
    vmem = pl.BlockSpec(memory_space=pltpu.VMEM)
    smem = pl.BlockSpec(memory_space=pltpu.SMEM)
    hbm = pl.BlockSpec(memory_space=pltpu.HBM)
    f32, bf16 = jnp.float32, jnp.bfloat16
    final, errors = pl.pallas_call(
        functools.partial(kernel, n, pix, width, depth, direct),
        out_shape=(jax.ShapeDtypeStruct(out_shape, f32), jax.ShapeDtypeStruct((ROUNDS, ITERS, 1), f32)),
        in_specs=[hbm, smem, smem, smem, hbm, hbm, hbm, hbm, hbm],
        out_specs=(vmem, vmem),
        scratch_shapes=[
            pltpu.VMEM(sent.shape, f32),
            pltpu.VMEM((lat, ch), bf16),
            pltpu.VMEM((lat, ch), bf16),
            pltpu.VMEM((ch, ch), f32),
            pltpu.VMEM((ch, ch), bf16),
            pltpu.VMEM((2 * ch, BASE), f32),
            pltpu.VMEM((n, lat, width), f32),
            pltpu.VMEM((n, 8, width), f32),
            pltpu.VMEM((n, lat, width), f32),
            pltpu.VMEM((n, ROUNDS * ITERS, LANES), f32),
            pltpu.VMEM((n, 1, LANES), f32),
            pltpu.VMEM((n, 1, LANES), f32),
            pltpu.VMEM((ch + 32, depth), bf16),
            pltpu.VMEM((ch, ch), bf16),
            pltpu.VMEM((8, ch), f32),
            pltpu.VMEM((8, ch), f32),
            pltpu.VMEM((ROUNDS * n, 8, LANES), f32),
            pltpu.VMEM((ROUNDS * n, 8, LANES), f32),
            pltpu.SemaphoreType.DMA((6,)),
        ] + [pltpu.SemaphoreType.DMA((n,))] * 6,
        compiler_params=pltpu.CompilerParams(
            collective_id=0, has_side_effects=True, vmem_limit_bytes=67043328),
        name="picard",
    )(sent, t_sched, advances, jnp.asarray(alpha_table()), in_weight.T, out_weight, time_weight, mid_weight,
      jnp.asarray(trig_tables(time_weight.shape[1])))
    if not direct:
        final = final[:, :, :pix].transpose(1, 0, 2).reshape(states.shape)
    return final, errors


def solution(mesh):
    in_specs = (P(("groups", "steps"), None, None), P("groups"), P("groups"), P(), P(), P(), P())
    out_specs = (P(("groups", "steps"), None, None), P("groups", None, "steps"))
    return jax.shard_map(shards, mesh=mesh, in_specs=in_specs, out_specs=out_specs, check_vma=False)
```

profile of v0, /device:TPU:0, one launch (start us, length us, event | category | flops | bytes accessed | tf_op | source)
XLA Modules:
  0.0 41.4 jit_solution(1174170519360940201)
XLA Ops:
  0.6 37.9 %picard.1 = (f32[1,4,4096]{2,1,0:T(4,128)}, f32[2,4,1]{2,1,0:T(4,128)}) custom-call(f32[1,4,4096]{2,1,0:T(4,128)} %states_hbm.1, s32[33]{0:T(128)} %sched_ref.1, s32[2]{0:T(128)} %adv_ref.1, f32[1000]{0:T(1024)} %constant.4.clone.alpha_ref, bf16[4,320]{1,0:T(4,128)(2,1)} %bitcast.1, bf16[4,320]{1,0:T(4,128)(2,1)} %outw_hbm.1, f32[320,320]{1,0:T(8,128)} %timew_hbm.1, ...), custom_call_target="tpu_custom_call" | custom-call | tf_op jit(solution)/shard_map/picard/pallas_call | solution.py:286
  38.6 1.3 %copy.11 = f32[2,4,1]{1,2,0:T(1,128)} copy(f32[2,4,1]{2,1,0:T(4,128)} %get-tuple-element.3) | data formatting | bytes 64 | tf_op jit(solution)/shard_map/picard/pallas_call | solution.py:286
  39.9 1.5 %copy.13 = f32[1,4,4096]{2,1,0:T(4,128)} copy(f32[1,4,4096]{2,1,0:T(4,128)} %get-tuple-element.6) | data formatting | bytes 131072
where the time goes:
time: 41.6 us; the launch traced here: 41.4 us
  Pallas kernels  37.9 us (91%)
  local copies, waits for them, and re-layouts  2.8 us (7%)
  between operations  0.64 us (2%)
    pallas_call x1, Pallas kernels, shards(): pl.pallas_call(functools.partial(kernel, n, pix, width, depth, direct), o...  37.9 us
    unnamed x1, local copies, waits for them, and re-layouts  1.47 us
    pallas_call x1, local copies, waits for them, and re-layouts, shards(): pl.pallas_call(functools.partial(kernel, n, pix, width, depth, direct), o...  1.33 us

commit v1 on v0

--- a/solution.py
+++ b/solution.py
@@ -15,7 +15,10 @@
 LANES = 128
 BASE = 32
 XROWS = 16
-GROUP_MOST = 15
+TILE = 256
+LAG_MIXED = 1
+LAG_NOISE = 3
+VECTOR_ROWS = 112
 
 
 def alpha_table():
@@ -41,10 +44,11 @@
 
 
 def kernel(
-    n, pix, width, depth, direct,
+    n, pix, width, depth, direct, vector_rows, fused,
     states_hbm, sched_ref, adv_ref, alpha_ref, inw_hbm, outw_hbm, timew_hbm, midw_hbm, trig_hbm,
     out_ref, err_ref,
-    states_ref, inw_ref, outw_ref, timew, midw, trig, xin, xs, fin, errs, elines, erecv, lhs, mid, outw, inw, coef_one, coef_two,
+    states_ref, inw_ref, outw_ref, timew, midw, trig, xin, xs, fin, errs, elines, erecv, lhs, mid, outs, outw, inw, coef_one, coef_two,
+    in_table, time_table, linear_in, linear_time,
     local, in_send, in_recv, out_send, out_recv, err_send, err_recv,
 ):
     lat = outw_ref.shape[0]
@@ -147,50 +151,83 @@
     part = jnp.where(lane < span, top, jnp.where(lane < 2 * span, middle, bottom))
     part = jnp.where(member >= 0, part, 0.0)
     left = spread + part
-    lhs[0:ch, :] = left.astype(bf16)
-    mid[...] = (midw[...].astype(f32) * 0.5).astype(bf16)
+    matrix_rows = ch - vector_rows
     outw[...] = jnp.zeros_like(outw)
     outw[0:lat, :] = outw_ref[...].astype(f32)
-    linear = 2.0 * jnp.dot(outw[...], left, precision=exact, preferred_element_type=f32)
-    linear_top = linear.astype(bf16).astype(f32)
-    linear_rest = linear - linear_top
-    linear_middle = linear_rest.astype(bf16).astype(f32)
-    linear_bottom = linear_rest - linear_middle
-    lhs[ch:ch + 32, :] = jnp.concatenate(
-        [linear_top, linear_middle, linear_bottom, jnp.zeros_like(linear)], axis=0).astype(bf16)
-
-    xs[...] = jnp.zeros_like(xs)
+    half_mid = (midw[...].astype(f32) * 0.5).astype(bf16)
+    padded_out = jnp.concatenate([outw[...], jnp.zeros_like(outw[...])], axis=0).astype(bf16)
+    narrow = lambda rows, lanes: jnp.zeros((rows, lanes), bf16)
+    cuts_one = (0, TILE - LANES // 2, ch)
+    cuts_two = (0, LANES // 2, TILE - (ch - cuts_one[1]) + LANES // 2, ch)
+    if fused:
+        for part in range(2):
+            one = half_mid[:, cuts_one[part]:cuts_one[part + 1]]
+            two = padded_out[:, cuts_two[part]:cuts_two[part + 1]]
+            mid[part, 0:ch, :] = jnp.concatenate([one, narrow(ch, two.shape[1])], axis=1)
+            mid[part, ch:, :] = jnp.concatenate([narrow(16, one.shape[1]), two], axis=1)
+        lhs[0:16, 0:LANES] = padded_out[:, cuts_two[2]:]
+        lhs[0:16, LANES:] = narrow(16, depth)
+        lhs[16:, 0:LANES] = narrow(matrix_rows, LANES)
+        lhs[16:, LANES:] = left[0:matrix_rows].astype(bf16)
+    else:
+        mid[...] = half_mid
+        outs[...] = padded_out
+        lhs[...] = left[0:matrix_rows].astype(bf16)
+    whole = spread + jnp.where(member >= 0, embed, 0.0)
+    linear = 2.0 * jnp.dot(outw[...], whole, precision=exact, preferred_element_type=f32)
+    for l in range(lat):
+        linear_in[l] = jnp.broadcast_to(linear[:, l:l + 1], (8, LANES))
+        if vector_rows:
+            in_table[l] = jnp.broadcast_to(whole[matrix_rows:, l:l + 1], (vector_rows, LANES))
+    for m in range(span):
+        at = XROWS + m
+        linear_time[m] = jnp.broadcast_to(linear[:, at:at + 1], (8, LANES))
+        if vector_rows:
+            time_table[m] = jnp.broadcast_to(whole[matrix_rows:, at:at + 1], (vector_rows, LANES))
+
+    xs[0] = jnp.zeros_like(xs[0])
     errs[...] = jnp.zeros_like(errs)
     if direct:
-        xs[me, 0:lat, :] = states_ref[0, :, pl.ds(pl.multiple_of(me * pix, LANES), pix)]
+        xs[0, me, 0:lat, :] = states_ref[0, :, pl.ds(pl.multiple_of(me * pix, LANES), pix)]
     else:
-        xs[me, 0:lat, :] = states_ref[me]
+        xs[0, me, 0:lat, :] = states_ref[me]
 
     def arrived(d):
         in_copy(d, d).wait_recv()
-        xs[d, 0:lat, :] = xin[d]
+        xs[0, d, 0:lat, :] = xin[d]
 
     each_peer(arrived)
 
     hot_row = lax.broadcasted_iota(jnp.int32, (depth - XROWS, LANES), 0)
     hot_member = jnp.where(hot_row < 3 * span, lax.rem(hot_row, span), -1)
-    outs = outw[...].astype(bf16)
     wide = lambda tile: jnp.concatenate([tile] * (width // LANES), axis=1) if width > LANES else tile
 
-    def first(x, m):
+    def swish(half):
+        return half + half * jnp.tanh(half)
+
+    join = lambda parts: parts[0] if len(parts) == 1 else jnp.concatenate(parts, axis=1)
+    tiles = [slice(start, start + LANES) for start in range(0, width, LANES)]
+
+    def affine(base, slopes, x, tile):
+        total = base
+        for l in range(lat):
+            total = total + slopes[l] * x[l:l + 1, tile]
+        return total
+
+    def column(x, m):
         hot = wide((hot_member == m).astype(f32).astype(bf16))
         padded = jnp.concatenate([x, jnp.zeros((XROWS - 8, width), f32)], axis=0).astype(bf16)
-        both = jnp.dot(lhs[...], jnp.concatenate([padded, hot], axis=0), preferred_element_type=f32)
-        pre = both[0:ch]
-        tail = both[ch:ch + 8] + both[ch + 8:ch + 16] + both[ch + 16:ch + 24]
-        return tail, (pre + pre * jnp.tanh(pre)).astype(bf16)
-
-    def second(tail, hidden):
-        mixed = jnp.dot(mid[...], hidden, preferred_element_type=f32)
-        return tail, (mixed + mixed * jnp.tanh(mixed)).astype(bf16)
-
-    def third(tail, hidden):
-        return tail + jnp.dot(outs, hidden, preferred_element_type=f32)
+        return jnp.concatenate([padded, hot], axis=0)
+
+    def vector_part(x, m):
+        rounded = x.astype(bf16).astype(f32)
+        tail = join([affine(linear_time[m], linear_in, rounded, tile) for tile in tiles])
+        if not vector_rows:
+            return tail, None
+        return tail, join([swish(affine(time_table[m], in_table, rounded, tile).astype(bf16)) for tile in tiles])
+
+    def product(weights, values):
+        return jnp.dot(weights, values, preferred_element_type=f32)
 
     def note_error(row, k, change):
         square = change * change
@@ -201,47 +238,113 @@
             total = total + square[:, start:start + LANES]
         errs[k, pl.ds(row, 1), :] = jnp.sum(total, axis=0, keepdims=True)
 
-    def one_round(r, carry):
-        def some(row, ks, running):
-            count = len(ks)
-            olds = [xs[k] for k in ks]
-            ones = [None] * count
-            twos = [None] * count
-            noises = [None] * count
-            for step in range(count + 2):
-                if step < count:
-                    ones[step] = first(olds[step], r * n + ks[step])
-                if 0 <= step - 1 < count:
-                    twos[step - 1] = second(*ones[step - 1])
-                if 0 <= step - 2 < count:
-                    noises[step - 2] = third(*twos[step - 2])
-            for j, k in enumerate(ks):
-                m = r * n + k
-                note_error(row, k, running - olds[j])
-                xs[k] = running
-                running = running + (wide(coef_one[m]) * olds[j] + wide(coef_two[m]) * noises[j])
-            return running
-
+    def moved(r, m_at, old, noise):
+        return wide(coef_one[m_at]) * old + wide(coef_two[m_at]) * noise
+
+    def flat_round(r):
+        todo = [(i, k) for i in range(ITERS) for k in range(i, n - 1)]
+        groups = [todo[j:j + 2] for j in range(0, len(todo), 2)]
+        count = len(groups)
+        tails, hidden, late, running = {}, {}, {}, {}
+
+        def finish(i, k, noise):
+            row = r * ITERS + i
+            old = xs[i, k]
+            if k == i:
+                running[i] = old
+                xs[ITERS, k] = old
+            running[i] = running[i] + moved(r, r * n + k, old, noise)
+            note_error(row, k + 1, running[i] - xs[i, k + 1])
+            xs[i + 1, k + 1] = running[i]
+
+        def pad(values, lanes):
+            return values if values.shape[1] == lanes else jnp.concatenate(
+                [values, jnp.zeros((values.shape[0], lanes - values.shape[1]), bf16)], axis=1)
+
+        for step in range(count + LAG_NOISE):
+            new, second, third = step, step - LAG_MIXED, step - LAG_NOISE
+            has_new, has_second, has_third = new < count, 0 <= second < count, 0 <= third < count
+            sizes = [len(groups[g]) * width for g, there in ((new, has_new), (second, has_second), (third, has_third)) if there]
+            lanes = max(sizes)
+            noise = mixed = None
+            if has_new:
+                now, extras, ends = [], [], []
+                for i, k in groups[new]:
+                    x = xs[i, k]
+                    now.append(column(x, r * n + k))
+                    tail, extra = vector_part(x, r * n + k)
+                    ends.append(tail)
+                    extras.append(extra)
+                tails[new] = ends
+                new_rows = pad(join(now), lanes)
+            else:
+                new_rows = jnp.zeros((depth, lanes), bf16)
+            old_rows = pad(late[third], lanes) if has_third else jnp.zeros((ch, lanes), bf16)
+            mid_rows = pad(hidden[second], lanes) if has_second else jnp.zeros((ch, lanes), bf16)
+            if has_new or has_third:
+                begin = 0 if has_third else 16
+                end = lhs.shape[0] if has_new else 16
+                both = product(lhs[begin:end], jnp.concatenate([old_rows[cuts_two[2]:], new_rows], axis=0))
+                if has_new:
+                    hid = swish(both[16 - begin:, 0:len(groups[new]) * width].astype(bf16))
+                    hidden[new] = jnp.concatenate([hid, join(extras)], axis=0) if vector_rows else hid
+                if has_third:
+                    noise = both[0:8]
+            if has_second or has_third:
+                begin = 0 if has_second else ch
+                end = ch + 16 if has_third else ch
+                for part in range(2):
+                    values = jnp.concatenate([
+                        mid_rows[cuts_one[part]:cuts_one[part + 1]], old_rows[cuts_two[part]:cuts_two[part + 1]]], axis=0)
+                    both = product(mid[part, begin:end], values)
+                    if has_second:
+                        mixed = both[0:ch] if mixed is None else mixed + both[0:ch]
+                    if has_third:
+                        noise = noise + both[ch - begin:ch - begin + 8]
+            if has_second:
+                late[second] = swish(mixed[:, 0:len(groups[second]) * width].astype(bf16))
+                del hidden[second]
+            if has_third:
+                for j, (i, k) in enumerate(groups[third]):
+                    finish(i, k, tails[third][j] + noise[:, j * width:(j + 1) * width])
+                del late[third]
+
+    def rolled_round(r):
         for i in range(ITERS):
             row = r * ITERS + i
-            if n <= GROUP_MOST + 1:
-                running = some(row, list(range(i, n - 1)), xs[i])
-            else:
-                running = lax.fori_loop(i, n - 1, lambda k, held: some(row, [k], held), xs[i])
-            note_error(row, n - 1, running - xs[n - 1])
-            xs[n - 1] = running
+
+            def body(k, running):
+                old = xs[0, k]
+                tail, _ = vector_part(old, r * n + k)
+                hid = swish(product(lhs[...], column(old, r * n + k)).astype(bf16))
+                noise = tail + product(outs[...], swish(product(mid[...], hid).astype(bf16)))[0:8]
+                note_error(row, k, running - old)
+                xs[0, k] = running
+                return running + moved(r, r * n + k, old, noise)
+
+            running = lax.fori_loop(i, n - 1, body, xs[0, i])
+            note_error(row, n - 1, running - xs[0, n - 1])
+            xs[0, n - 1] = running
+
+    def one_round(r, carry):
         advance = adv_ref[r]
-
-        def shift(k, carry):
-            xs[k] = xs[jnp.minimum(k + advance, n - 1)]
-            return carry
-
-        lax.fori_loop(0, n, shift, 0, unroll=4)
+        if fused:
+            flat_round(r)
+            for k in range(n):
+                xs[0, k] = xs[ITERS, jnp.minimum(k + advance, n - 1)]
+        else:
+            rolled_round(r)
+
+            def shift(k, carry):
+                xs[0, k] = xs[0, jnp.minimum(k + advance, n - 1)]
+                return carry
+
+            lax.fori_loop(0, n, shift, 0, unroll=4)
         return carry
 
     lax.fori_loop(0, ROUNDS, one_round, 0)
     for k in range(n):
-        fin[k] = xs[k, 0:lat, :]
+        fin[k] = xs[0, k, 0:lat, :]
     each_peer(lambda d: out_copy(d, me).start())
     cells = (ROUNDS * ITERS, LANES)
     diagonal = lax.broadcasted_iota(jnp.int32, cells, 0) == lax.broadcasted_iota(jnp.int32, cells, 1)
@@ -273,6 +376,10 @@
     direct = pix % LANES == 0
     width = round_up(pix, LANES)
     depth = round_up(XROWS + 3 * ROUNDS * n, LANES)
+    fused = (
+        n <= 16 and width == TILE and ch == TILE + LANES // 2 and depth == LANES
+        and (n - ITERS + 1) // 2 > LAG_NOISE and VECTOR_ROWS < ch)
+    vector_rows = VECTOR_ROWS if fused else 0
     if direct:
         sent = states
         out_shape = states.shape
@@ -284,7 +391,7 @@
     hbm = pl.BlockSpec(memory_space=pltpu.HBM)
     f32, bf16 = jnp.float32, jnp.bfloat16
     final, errors = pl.pallas_call(
-        functools.partial(kernel, n, pix, width, depth, direct),
+        functools.partial(kernel, n, pix, width, depth, direct, vector_rows, fused),
         out_shape=(jax.ShapeDtypeStruct(out_shape, f32), jax.ShapeDtypeStruct((ROUNDS, ITERS, 1), f32)),
         in_specs=[hbm, smem, smem, smem, hbm, hbm, hbm, hbm, hbm],
         out_specs=(vmem, vmem),
@@ -296,16 +403,21 @@
             pltpu.VMEM((ch, ch), bf16),
             pltpu.VMEM((2 * ch, BASE), f32),
             pltpu.VMEM((n, lat, width), f32),
-            pltpu.VMEM((n, 8, width), f32),
+            pltpu.VMEM((ITERS + 1, n, 8, width), f32),
             pltpu.VMEM((n, lat, width), f32),
             pltpu.VMEM((n, ROUNDS * ITERS, LANES), f32),
             pltpu.VMEM((n, 1, LANES), f32),
             pltpu.VMEM((n, 1, LANES), f32),
-            pltpu.VMEM((ch + 32, depth), bf16),
-            pltpu.VMEM((ch, ch), bf16),
+            pltpu.VMEM((16 + ch - vector_rows, LANES + depth) if fused else (ch, depth), bf16),
+            pltpu.VMEM((2, ch + 16, TILE) if fused else (ch, ch), bf16),
+            pltpu.VMEM((16, ch), bf16),
             pltpu.VMEM((8, ch), f32),
             pltpu.VMEM((8, ch), f32),
             pltpu.VMEM((ROUNDS * n, 8, LANES), f32),
+            pltpu.VMEM((ROUNDS * n, 8, LANES), f32),
+            pltpu.VMEM((lat, max(vector_rows, 8), LANES), f32),
+            pltpu.VMEM((ROUNDS * n, max(vector_rows, 8), LANES), f32),
+            pltpu.VMEM((lat, 8, LANES), f32),
             pltpu.VMEM((ROUNDS * n, 8, LANES), f32),
             pltpu.SemaphoreType.DMA((6,)),
         ] + [pltpu.SemaphoreType.DMA((n,))] * 6,

time: 41.6 us -> 37.3 us (0.90)
  Pallas kernels: 37.9 us -> 33.6 us
    pallas_call x1, Pallas kernels: 37.9 us -> 33.6 us  [shards(): pl.pallas_call(functools.partial(kernel, n, pix, width, depth, direct, ve...]
where the time goes in v1:
time: 37.3 us; the launch traced here: 37 us
  Pallas kernels  33.6 us (90%)
  local copies, waits for them, and re-layouts  2.8 us (8%)
  between operations  0.64 us (2%)
    pallas_call x1, Pallas kernels, shards(): pl.pallas_call(functools.partial(kernel, n, pix, width, depth, direct, ve...  33.6 us
    unnamed x1, local copies, waits for them, and re-layouts  1.47 us
    pallas_call x1, local copies, waits for them, and re-layouts, shards(): pl.pallas_call(functools.partial(kernel, n, pix, width, depth, direct, ve...  1.33 us

profile of v1, /device:TPU:0, one launch (start us, length us, event | category | flops | bytes accessed | tf_op | source)
XLA Modules:
  0.0 37.0 jit_solution(10753426529650974690)
XLA Ops:
  0.6 33.6 %picard.1 = (f32[1,4,4096]{2,1,0:T(4,128)}, f32[2,4,1]{2,1,0:T(4,128)}) custom-call(f32[1,4,4096]{2,1,0:T(4,128)} %states_hbm.1, s32[33]{0:T(128)} %sched_ref.1, s32[2]{0:T(128)} %adv_ref.1, f32[1000]{0:T(1024)} %constant.4.clone.alpha_ref, bf16[4,320]{1,0:T(4,128)(2,1)} %bitcast.1, bf16[4,320]{1,0:T(4,128)(2,1)} %outw_hbm.1, f32[320,320]{1,0:T(8,128)} %timew_hbm.1, ...), custom_call_target="tpu_custom_call" | custom-call | tf_op jit(solution)/shard_map/picard/pallas_call | solution.py:393
  34.2 1.3 %copy.11 = f32[2,4,1]{1,2,0:T(1,128)} copy(f32[2,4,1]{2,1,0:T(4,128)} %get-tuple-element.3) | data formatting | bytes 64 | tf_op jit(solution)/shard_map/picard/pallas_call | solution.py:393
  35.6 1.5 %copy.13 = f32[1,4,4096]{2,1,0:T(4,128)} copy(f32[1,4,4096]{2,1,0:T(4,128)} %get-tuple-element.6) | data formatting | bytes 131072

commit v2 on v1

--- a/solution.py
+++ b/solution.py
@@ -18,6 +18,7 @@
 TILE = 256
 LAG_MIXED = 1
 LAG_NOISE = 3
+VMEM_BYTES = 40 << 20
 VECTOR_ROWS = 112
 
 
@@ -45,9 +46,9 @@
 
 def kernel(
     n, pix, width, depth, direct, vector_rows, fused,
-    states_hbm, sched_ref, adv_ref, alpha_ref, inw_hbm, outw_hbm, timew_hbm, midw_hbm, trig_hbm,
+    states_hbm, sched_hbm, adv_hbm, alpha_hbm, inw_hbm, outw_hbm, timew_hbm, midw_hbm, trig_hbm,
     out_ref, err_ref,
-    states_ref, inw_ref, outw_ref, timew, midw, trig, xin, xs, fin, errs, elines, erecv, lhs, mid, outs, outw, inw, coef_one, coef_two,
+    sched_ref, adv_ref, alpha_ref, states_ref, inw_ref, outw_ref, timew, midw, trig, xin, xs, fin, errs, elines, erecv, lhs, mid, outs, outw, inw, coef_one, coef_two,
     in_table, time_table, linear_in, linear_time,
     local, in_send, in_recv, out_send, out_recv, err_send, err_recv,
 ):
@@ -94,18 +95,23 @@
             def _(hop):
                 act(peer(hop))
 
+    barrier = pltpu.get_barrier_semaphore()
+    each_peer(lambda d: pl.semaphore_signal(
+        barrier, inc=1, device_id={"steps": d}, device_id_type=pl.DeviceIdType.MESH))
     loads = [
         pltpu.make_async_copy(source_ref, held, local.at[j])
         for j, (source_ref, held) in enumerate((
-            (states_hbm, states_ref), (trig_hbm, trig), (timew_hbm, timew), (midw_hbm, midw),
-            (inw_hbm, inw_ref), (outw_hbm, outw_ref)))
+            (states_hbm, states_ref), (sched_hbm, sched_ref), (adv_hbm, adv_ref), (alpha_hbm, alpha_ref),
+            (trig_hbm, trig), (timew_hbm, timew), (midw_hbm, midw), (inw_hbm, inw_ref), (outw_hbm, outw_ref)))
     ]
     for load in loads:
         load.start()
-    barrier = pltpu.get_barrier_semaphore()
-    each_peer(lambda d: pl.semaphore_signal(
-        barrier, inc=1, device_id={"steps": d}, device_id_type=pl.DeviceIdType.MESH))
-
+    loads[0].wait()
+    pl.semaphore_wait(barrier, n - 1)
+    each_peer(lambda d: in_copy(d, me).start())
+
+    for load in loads[1:4]:
+        load.wait()
     lane = lax.broadcasted_iota(jnp.int32, (1, depth), 1) - XROWS
     member = jnp.where((lane >= 0) & (lane < 3 * span), lax.rem(jnp.maximum(lane, 0), span), -1)
     advance_one = adv_ref[0]
@@ -121,17 +127,13 @@
         coef_two[m] = two
         return jnp.where(member == m, now, stamps)
 
-    stamps = lax.fori_loop(0, span, coefficients, jnp.zeros((1, depth), jnp.int32), unroll=4)
-
-    loads[0].wait()
-    pl.semaphore_wait(barrier, n - 1)
-    each_peer(lambda d: in_copy(d, me).start())
+    stamps = lax.fori_loop(0, span, coefficients, jnp.zeros((1, depth), jnp.int32), unroll=8)
 
     digit = lax.broadcasted_iota(jnp.int32, (BASE, depth), 0)
     hot_high = (digit == lax.shift_right_logical(stamps, 5)).astype(f32)
     hot_low = (digit == lax.bitwise_and(stamps, BASE - 1)).astype(f32)
     exact = lax.Precision.HIGHEST
-    for load in loads[1:]:
+    for load in loads[4:]:
         load.wait()
     high = jnp.dot(trig[0:ch], hot_high, precision=exact, preferred_element_type=f32)
     low = jnp.dot(trig[ch:], hot_low, precision=exact, preferred_element_type=f32)
@@ -359,13 +361,24 @@
     erecv[me] = elines[me]
     each_peer(lambda d: err_copy(d, d).wait_recv())
     sums = lax.fori_loop(0, n, lambda k, total: total + erecv[k], jnp.zeros((1, LANES), f32), unroll=4)
-    means = jnp.sum(jnp.where(diagonal, sums, 0.0), axis=1, keepdims=True) * (1.0 / (lat * n * pix))
+    means = sums * (1.0 / (lat * n * pix))
     for r in range(ROUNDS):
-        err_ref[r] = means[r * ITERS:(r + 1) * ITERS]
+        err_ref[r] = means[:, r * ITERS:(r + 1) * ITERS]
     each_peer(lambda d: out_copy(d, d).wait_recv())
     each_peer(lambda d: in_copy(d, me).wait_send())
     each_peer(lambda d: out_copy(d, me).wait_send())
     each_peer(lambda d: err_copy(d, me).wait_send())
+
+
+def closing(final_ref, errors_ref, final_out, errors_out, sems):
+    copies = [
+        pltpu.make_async_copy(final_ref, final_out, sems.at[0]),
+        pltpu.make_async_copy(errors_ref, errors_out, sems.at[1]),
+    ]
+    for copy in copies:
+        copy.start()
+    for copy in copies:
+        copy.wait()
 
 
 def shards(states, t_sched, advances, in_weight, time_weight, mid_weight, out_weight):
@@ -387,15 +400,17 @@
         sent = jnp.pad(states.reshape(lat, n, pix).transpose(1, 0, 2), ((0, 0), (0, 0), (0, width - pix)))
         out_shape = sent.shape
     vmem = pl.BlockSpec(memory_space=pltpu.VMEM)
-    smem = pl.BlockSpec(memory_space=pltpu.SMEM)
     hbm = pl.BlockSpec(memory_space=pltpu.HBM)
     f32, bf16 = jnp.float32, jnp.bfloat16
     final, errors = pl.pallas_call(
         functools.partial(kernel, n, pix, width, depth, direct, vector_rows, fused),
-        out_shape=(jax.ShapeDtypeStruct(out_shape, f32), jax.ShapeDtypeStruct((ROUNDS, ITERS, 1), f32)),
-        in_specs=[hbm, smem, smem, smem, hbm, hbm, hbm, hbm, hbm],
+        out_shape=(pltpu.VMEM(out_shape, f32), pltpu.VMEM((ROUNDS, 1, ITERS), f32)),
+        in_specs=[hbm] * 9,
         out_specs=(vmem, vmem),
         scratch_shapes=[
+            pltpu.SMEM(t_sched.shape, jnp.int32),
+            pltpu.SMEM(advances.shape, jnp.int32),
+            pltpu.SMEM((TSTEPS,), f32),
             pltpu.VMEM(sent.shape, f32),
             pltpu.VMEM((lat, ch), bf16),
             pltpu.VMEM((lat, ch), bf16),
@@ -419,13 +434,24 @@
             pltpu.VMEM((ROUNDS * n, max(vector_rows, 8), LANES), f32),
             pltpu.VMEM((lat, 8, LANES), f32),
             pltpu.VMEM((ROUNDS * n, 8, LANES), f32),
-            pltpu.SemaphoreType.DMA((6,)),
+            pltpu.SemaphoreType.DMA((9,)),
         ] + [pltpu.SemaphoreType.DMA((n,))] * 6,
         compiler_params=pltpu.CompilerParams(
-            collective_id=0, has_side_effects=True, vmem_limit_bytes=67043328),
+            collective_id=0, has_side_effects=True, vmem_limit_bytes=VMEM_BYTES),
         name="picard",
-    )(sent, t_sched, advances, jnp.asarray(alpha_table()), in_weight.T, out_weight, time_weight, mid_weight,
-      jnp.asarray(trig_tables(time_weight.shape[1])))
+    )(*[pltpu.with_memory_space_constraint(held, pltpu.HBM) for held in (
+        sent, t_sched, advances, jnp.asarray(alpha_table()), in_weight.T, out_weight, time_weight, mid_weight,
+        jnp.asarray(trig_tables(time_weight.shape[1])))])
+    final, errors = pl.pallas_call(
+        closing,
+        out_shape=(pltpu.HBM(out_shape, f32), pltpu.HBM((ROUNDS, 1, ITERS), f32)),
+        in_specs=[vmem, vmem],
+        out_specs=(hbm, hbm),
+        scratch_shapes=[pltpu.SemaphoreType.DMA((2,))],
+        compiler_params=pltpu.CompilerParams(vmem_limit_bytes=1 << 20),
+        name="closing",
+    )(pltpu.with_memory_space_constraint(final, pltpu.VMEM), pltpu.with_memory_space_constraint(errors, pltpu.VMEM))
+    errors = errors.transpose(0, 2, 1)
     if not direct:
         final = final[:, :, :pix].transpose(1, 0, 2).reshape(states.shape)
     return final, errors

time: 37.3 us -> 33.7 us (0.903)
  local copies, waits for them, and re-layouts: 2.8 us -> 0 us
  Pallas kernels: 33.6 us -> 32.9 us
    unnamed x1 -> x0, local copies, waits for them, and re-layouts: 1.47 us -> none
    pallas_call x1, Pallas kernels: 33.6 us -> 32.3 us  [shards(): pl.pallas_call(functools.partial(kernel, n, pix, width, depth, direct, ve...]
    pallas_call x1 -> x0, local copies, waits for them, and re-layouts: 1.33 us -> none  [shards(): pl.pallas_call(functools.partial(kernel, n, pix, width, depth, direct, ve...]
    pallas_call x0 -> x1, Pallas kernels: none -> 0.65 us  [shards(): pl.pallas_call(closing, out_shape=(pltpu.HBM(out_shape, f32), pltpu.HBM((...]
where the time goes in v2:
time: 33.7 us; the launch traced here: 33.6 us
  Pallas kernels  32.9 us (98%)
  between operations  0.64 us (2%)
    pallas_call x1, Pallas kernels, shards(): pl.pallas_call(functools.partial(kernel, n, pix, width, depth, direct, ve...  32.3 us

profile of v2, /device:TPU:0, one launch (start us, length us, event | category | flops | bytes accessed | tf_op | source)
XLA Modules:
  0.0 33.6 jit_solution(15629144968184672129)
XLA Ops:
  0.6 32.3 %picard.1 = (f32[1,4,4096]{2,1,0:T(4,128)S(1)}, f32[2,1,4]{2,1,0:T(1,128)S(1)}) custom-call(f32[1,4,4096]{2,1,0:T(4,128)} %states_hbm.1, s32[33]{0:T(128)} %sched_hbm.1, s32[2]{0:T(128)} %adv_hbm.1, f32[1000]{0:T(1024)} %constant.4.clone.alpha_hbm, bf16[4,320]{1,0:T(4,128)(2,1)} %bitcast.4, bf16[4,320]{1,0:T(4,128)(2,1)} %outw_hbm.1, f32[320,320]{1,0:T(8,128)} %timew_hbm.1, ...), custom_call_target="tpu_custom_call" | custom-call | tf_op jit(solution)/shard_map/picard/pallas_call | solution.py:405
  32.9 0.7 %closing.1 = (f32[1,4,4096]{2,1,0:T(4,128)}, f32[2,1,4]{2,1,0:T(1,128)}) custom-call(f32[1,4,4096]{2,1,0:T(4,128)S(1)} %get-tuple-element.6.final_ref, f32[2,1,4]{2,1,0:T(1,128)S(1)} %get-tuple-element.7.errors_ref), custom_call_target="tpu_custom_call" | custom-call | tf_op jit(solution)/shard_map/closing/pallas_call | solution.py:445

commit v3 on v2

--- a/solution.py
+++ b/solution.py
@@ -19,7 +19,7 @@
 LAG_MIXED = 1
 LAG_NOISE = 3
 VMEM_BYTES = 40 << 20
-VECTOR_ROWS = 112
+VECTOR_ROWS = 176
 
 
 def alpha_table():
@@ -48,9 +48,9 @@
     n, pix, width, depth, direct, vector_rows, fused,
     states_hbm, sched_hbm, adv_hbm, alpha_hbm, inw_hbm, outw_hbm, timew_hbm, midw_hbm, trig_hbm,
     out_ref, err_ref,
-    sched_ref, adv_ref, alpha_ref, states_ref, inw_ref, outw_ref, timew, midw, trig, xin, xs, fin, errs, elines, erecv, lhs, mid, outs, outw, inw, coef_one, coef_two,
-    in_table, time_table, linear_in, linear_time,
-    local, in_send, in_recv, out_send, out_recv, err_send, err_recv,
+    sched_ref, adv_ref, alpha_ref, states_ref, inw_ref, outw_ref, timew, midw, trig, xin, xs, fin, final_in, errs, lhs, mid, outs, outw, inw, coef_one, coef_two,
+    in_table, time_table, linear_in, linear_time, hot_table,
+    local, in_send, in_recv, out_send, out_recv,
 ):
     lat = outw_ref.shape[0]
     ch = midw.shape[0]
@@ -59,18 +59,20 @@
     f32, bf16 = jnp.float32, jnp.bfloat16
 
     def peer(hop):
-        return lax.rem(me + hop, n)
+        if n > 16 or n & (n - 1):
+            return lax.rem(me + hop, n)
+        other = me
+        for bit in range(n.bit_length() - 1):
+            if hop >> bit & 1:
+                digit = lax.rem(lax.div(me, 1 << bit), 2)
+                other = other + (1 << bit) * (1 - 2 * digit)
+        return other
 
     def source(d):
         if direct:
             return states_ref.at[0, :, pl.ds(pl.multiple_of(d * pix, LANES), pix)]
         return states_ref.at[d]
 
-    def target(d):
-        if direct:
-            return out_ref.at[0, :, pl.ds(pl.multiple_of(d * pix, LANES), pix)]
-        return out_ref.at[d]
-
     def in_copy(d, slot):
         return pltpu.make_async_remote_copy(
             src_ref=source(d), dst_ref=xin.at[slot], send_sem=in_send.at[d], recv_sem=in_recv.at[slot],
@@ -78,33 +80,29 @@
 
     def out_copy(d, slot):
         return pltpu.make_async_remote_copy(
-            src_ref=fin.at[d], dst_ref=target(slot), send_sem=out_send.at[d], recv_sem=out_recv.at[slot],
-            device_id={"steps": d}, device_id_type=pl.DeviceIdType.MESH)
-
-    def err_copy(d, slot):
-        return pltpu.make_async_remote_copy(
-            src_ref=elines.at[d], dst_ref=erecv.at[slot], send_sem=err_send.at[d], recv_sem=err_recv.at[slot],
+            src_ref=fin.at[d], dst_ref=final_in.at[slot], send_sem=out_send.at[d], recv_sem=out_recv.at[slot],
             device_id={"steps": d}, device_id_type=pl.DeviceIdType.MESH)
 
     def each_peer(act):
         if n <= 16:
-            for hop in range(1, n):
+            for hop in reversed(range(1, n)):
                 act(peer(hop))
         else:
             @pl.loop(1, n)
             def _(hop):
                 act(peer(hop))
 
-    barrier = pltpu.get_barrier_semaphore()
-    each_peer(lambda d: pl.semaphore_signal(
-        barrier, inc=1, device_id={"steps": d}, device_id_type=pl.DeviceIdType.MESH))
     loads = [
         pltpu.make_async_copy(source_ref, held, local.at[j])
         for j, (source_ref, held) in enumerate((
             (states_hbm, states_ref), (sched_hbm, sched_ref), (adv_hbm, adv_ref), (alpha_hbm, alpha_ref),
             (trig_hbm, trig), (timew_hbm, timew), (midw_hbm, midw), (inw_hbm, inw_ref), (outw_hbm, outw_ref)))
     ]
-    for load in loads:
+    loads[0].start()
+    barrier = pltpu.get_barrier_semaphore()
+    each_peer(lambda d: pl.semaphore_signal(
+        barrier, inc=1, device_id={"steps": d}, device_id_type=pl.DeviceIdType.MESH))
+    for load in loads[1:]:
         load.start()
     loads[0].wait()
     pl.semaphore_wait(barrier, n - 1)
@@ -140,9 +138,9 @@
     half = ch // 2
     cos_h, sin_h, cos_l, sin_l = high[:half], high[half:], low[:half], low[half:]
     feats = jnp.concatenate([cos_h * cos_l - sin_h * sin_l, sin_h * cos_l + cos_h * sin_l], axis=0)
-    embed = 0.5 * jnp.dot(timew[...], feats, precision=exact, preferred_element_type=f32)
+    embed = jnp.dot(timew[...], feats, precision=exact, preferred_element_type=f32)
     inw[...] = jnp.zeros_like(inw)
-    inw[0:lat, :] = inw_ref[...].astype(f32) * 0.5
+    inw[0:lat, :] = inw_ref[...].astype(f32)
     unit = (lax.broadcasted_iota(jnp.int32, (8, depth), 0) == lane + XROWS).astype(f32)
     spread = lax.dot_general(
         inw[...], unit, (((0,), (0,)), ((), ())), precision=exact, preferred_element_type=f32)
@@ -157,55 +155,81 @@
     outw[...] = jnp.zeros_like(outw)
     outw[0:lat, :] = outw_ref[...].astype(f32)
     half_mid = (midw[...].astype(f32) * 0.5).astype(bf16)
+    whole = spread + jnp.where(member >= 0, embed, 0.0)
+    linear = jnp.dot(outw[...], whole, precision=exact, preferred_element_type=f32)
+
+    def folded(high, low):
+        return jnp.concatenate([jnp.zeros_like(high), high + pltpu.roll(low, lat, axis=0)], axis=0).astype(bf16)
+
     padded_out = jnp.concatenate([outw[...], jnp.zeros_like(outw[...])], axis=0).astype(bf16)
     narrow = lambda rows, lanes: jnp.zeros((rows, lanes), bf16)
     cuts_one = (0, TILE - LANES // 2, ch)
     cuts_two = (0, LANES // 2, TILE - (ch - cuts_one[1]) + LANES // 2, ch)
     if fused:
+        both_out = jnp.dot(padded_out, half_mid, preferred_element_type=f32)[0:8]
+        both_top = both_out.astype(bf16).astype(f32)
+        passed = folded(both_top, both_out - both_top)
         for part in range(2):
             one = half_mid[:, cuts_one[part]:cuts_one[part + 1]]
             two = padded_out[:, cuts_two[part]:cuts_two[part + 1]]
             mid[part, 0:ch, :] = jnp.concatenate([one, narrow(ch, two.shape[1])], axis=1)
-            mid[part, ch:, :] = jnp.concatenate([narrow(16, one.shape[1]), two], axis=1)
+            through = passed[:, cuts_one[part]:cuts_one[part + 1]]
+            mid[part, ch:, :] = jnp.concatenate([through, two], axis=1)
         lhs[0:16, 0:LANES] = padded_out[:, cuts_two[2]:]
-        lhs[0:16, LANES:] = narrow(16, depth)
+        line_top = linear.astype(bf16).astype(f32)
+        line_rest = linear - line_top
+        line_middle = line_rest.astype(bf16).astype(f32)
+        line_bottom = line_rest - line_middle
+        line = jnp.where(lane < span, line_top, jnp.where(lane < 2 * span, line_middle, line_bottom))
+        lhs[0:16, LANES:] = folded(
+            jnp.where((member >= 0) | (lane < 0), line, 0.0), jnp.where(lane < 0, line_middle, 0.0))
         lhs[16:, 0:LANES] = narrow(matrix_rows, LANES)
         lhs[16:, LANES:] = left[0:matrix_rows].astype(bf16)
     else:
         mid[...] = half_mid
         outs[...] = padded_out
         lhs[...] = left[0:matrix_rows].astype(bf16)
-    whole = spread + jnp.where(member >= 0, embed, 0.0)
-    linear = 2.0 * jnp.dot(outw[...], whole, precision=exact, preferred_element_type=f32)
     for l in range(lat):
-        linear_in[l] = jnp.broadcast_to(linear[:, l:l + 1], (8, LANES))
+        if not fused:
+            linear_in[l] = jnp.broadcast_to(linear[:, l:l + 1], (8, LANES))
         if vector_rows:
             in_table[l] = jnp.broadcast_to(whole[matrix_rows:, l:l + 1], (vector_rows, LANES))
     for m in range(span):
         at = XROWS + m
-        linear_time[m] = jnp.broadcast_to(linear[:, at:at + 1], (8, LANES))
+        if not fused:
+            linear_time[m] = jnp.broadcast_to(linear[:, at:at + 1], (8, LANES))
         if vector_rows:
             time_table[m] = jnp.broadcast_to(whole[matrix_rows:, at:at + 1], (vector_rows, LANES))
 
-    xs[0] = jnp.zeros_like(xs[0])
+    hot_row = lax.broadcasted_iota(jnp.int32, (depth - XROWS, LANES), 0)
+    hot_member = jnp.where(hot_row < 3 * span, lax.rem(hot_row, span), -1)
+    if fused:
+        for m in range(span):
+            hot_table[m] = (hot_member == m).astype(f32).astype(bf16)
+    copies = 2 if fused else 1
+    if not fused:
+        xs[0] = jnp.zeros_like(xs[0])
     errs[...] = jnp.zeros_like(errs)
-    if direct:
-        xs[0, me, 0:lat, :] = states_ref[0, :, pl.ds(pl.multiple_of(me * pix, LANES), pix)]
-    else:
-        xs[0, me, 0:lat, :] = states_ref[me]
+
+    def place(d, values):
+        for copy in range(copies):
+            xs[0, d, copy * lat:(copy + 1) * lat, :] = values
+
+    place(me, states_ref[0, :, pl.ds(pl.multiple_of(me * pix, LANES), pix)] if direct else states_ref[me])
 
     def arrived(d):
         in_copy(d, d).wait_recv()
-        xs[0, d, 0:lat, :] = xin[d]
+        place(d, xin[d])
 
     each_peer(arrived)
 
-    hot_row = lax.broadcasted_iota(jnp.int32, (depth - XROWS, LANES), 0)
-    hot_member = jnp.where(hot_row < 3 * span, lax.rem(hot_row, span), -1)
     wide = lambda tile: jnp.concatenate([tile] * (width // LANES), axis=1) if width > LANES else tile
 
-    def swish(half):
-        return half + half * jnp.tanh(half)
+    def swish(full):
+        return full * jax.nn.sigmoid(full)
+
+    def bent(half):
+        return half * jnp.tanh(half)
 
     join = lambda parts: parts[0] if len(parts) == 1 else jnp.concatenate(parts, axis=1)
     tiles = [slice(start, start + LANES) for start in range(0, width, LANES)]
@@ -217,16 +241,17 @@
         return total
 
     def column(x, m):
-        hot = wide((hot_member == m).astype(f32).astype(bf16))
+        hot = wide(hot_table[m] if fused else (hot_member == m).astype(f32).astype(bf16))
         padded = jnp.concatenate([x, jnp.zeros((XROWS - 8, width), f32)], axis=0).astype(bf16)
         return jnp.concatenate([padded, hot], axis=0)
 
     def vector_part(x, m):
         rounded = x.astype(bf16).astype(f32)
-        tail = join([affine(linear_time[m], linear_in, rounded, tile) for tile in tiles])
-        if not vector_rows:
-            return tail, None
-        return tail, join([swish(affine(time_table[m], in_table, rounded, tile).astype(bf16)) for tile in tiles])
+        return join([swish(affine(time_table[m], in_table, rounded, tile).astype(bf16)) for tile in tiles])
+
+    def linear_part(x, m):
+        rounded = x.astype(bf16).astype(f32)
+        return join([affine(linear_time[m], linear_in, rounded, tile) for tile in tiles])
 
     def product(weights, values):
         return jnp.dot(weights, values, preferred_element_type=f32)
@@ -247,7 +272,7 @@
         todo = [(i, k) for i in range(ITERS) for k in range(i, n - 1)]
         groups = [todo[j:j + 2] for j in range(0, len(todo), 2)]
         count = len(groups)
-        tails, hidden, late, running = {}, {}, {}, {}
+        tails, hidden, late, running, straight = {}, {}, {}, {}, {}
 
         def finish(i, k, noise):
             row = r * ITERS + i
@@ -270,45 +295,45 @@
             lanes = max(sizes)
             noise = mixed = None
             if has_new:
-                now, extras, ends = [], [], []
+                now, extras = [], []
                 for i, k in groups[new]:
                     x = xs[i, k]
                     now.append(column(x, r * n + k))
-                    tail, extra = vector_part(x, r * n + k)
-                    ends.append(tail)
-                    extras.append(extra)
-                tails[new] = ends
+                    extras.append(vector_part(x, r * n + k))
                 new_rows = pad(join(now), lanes)
             else:
                 new_rows = jnp.zeros((depth, lanes), bf16)
             old_rows = pad(late[third], lanes) if has_third else jnp.zeros((ch, lanes), bf16)
             mid_rows = pad(hidden[second], lanes) if has_second else jnp.zeros((ch, lanes), bf16)
             if has_new or has_third:
-                begin = 0 if has_third else 16
                 end = lhs.shape[0] if has_new else 16
-                both = product(lhs[begin:end], jnp.concatenate([old_rows[cuts_two[2]:], new_rows], axis=0))
+                both = product(lhs[0:end], jnp.concatenate([old_rows[cuts_two[2]:], new_rows], axis=0))
                 if has_new:
-                    hid = swish(both[16 - begin:, 0:len(groups[new]) * width].astype(bf16))
+                    tails[new] = both[8:16]
+                    hid = swish(both[16:, 0:len(groups[new]) * width].astype(bf16))
                     hidden[new] = jnp.concatenate([hid, join(extras)], axis=0) if vector_rows else hid
                 if has_third:
                     noise = both[0:8]
             if has_second or has_third:
                 begin = 0 if has_second else ch
-                end = ch + 16 if has_third else ch
                 for part in range(2):
                     values = jnp.concatenate([
                         mid_rows[cuts_one[part]:cuts_one[part + 1]], old_rows[cuts_two[part]:cuts_two[part + 1]]], axis=0)
-                    both = product(mid[part, begin:end], values)
+                    both = product(mid[part, begin:], values)
                     if has_second:
                         mixed = both[0:ch] if mixed is None else mixed + both[0:ch]
+                        line = both[ch + 8:ch + 16]
+                        straight[second] = straight[second] + line if second in straight else line
                     if has_third:
                         noise = noise + both[ch - begin:ch - begin + 8]
             if has_second:
-                late[second] = swish(mixed[:, 0:len(groups[second]) * width].astype(bf16))
+                late[second] = bent(mixed[:, 0:len(groups[second]) * width].astype(bf16))
                 del hidden[second]
             if has_third:
                 for j, (i, k) in enumerate(groups[third]):
-                    finish(i, k, tails[third][j] + noise[:, j * width:(j + 1) * width])
+                    at = slice(j * width, (j + 1) * width)
+                    total = tails[third][:, at] + straight[third][:, at] + noise[:, at]
+                    finish(i, k, total + pltpu.roll(total, lat, axis=0))
                 del late[third]
 
     def rolled_round(r):
@@ -317,9 +342,10 @@
 
             def body(k, running):
                 old = xs[0, k]
-                tail, _ = vector_part(old, r * n + k)
+                tail = linear_part(old, r * n + k)
                 hid = swish(product(lhs[...], column(old, r * n + k)).astype(bf16))
-                noise = tail + product(outs[...], swish(product(mid[...], hid).astype(bf16)))[0:8]
+                half = product(mid[...], hid).astype(bf16)
+                noise = tail + product(outs[...], half + bent(half))[0:8]
                 note_error(row, k, running - old)
                 xs[0, k] = running
                 return running + moved(r, r * n + k, old, noise)
@@ -345,29 +371,28 @@
         return carry
 
     lax.fori_loop(0, ROUNDS, one_round, 0)
-    for k in range(n):
-        fin[k] = xs[0, k, 0:lat, :]
-    each_peer(lambda d: out_copy(d, me).start())
     cells = (ROUNDS * ITERS, LANES)
     diagonal = lax.broadcasted_iota(jnp.int32, cells, 0) == lax.broadcasted_iota(jnp.int32, cells, 1)
+    fin[...] = jnp.zeros_like(fin)
     for k in range(n):
         total = jnp.sum(errs[k], axis=1, keepdims=True)
-        elines[k] = jnp.sum(jnp.where(diagonal, total, 0.0), axis=0, keepdims=True)
-    each_peer(lambda d: err_copy(d, me).start())
-    if direct:
-        out_ref[0, :, pl.ds(pl.multiple_of(me * pix, LANES), pix)] = fin[me]
-    else:
-        out_ref[me] = fin[me]
-    erecv[me] = elines[me]
-    each_peer(lambda d: err_copy(d, d).wait_recv())
-    sums = lax.fori_loop(0, n, lambda k, total: total + erecv[k], jnp.zeros((1, LANES), f32), unroll=4)
-    means = sums * (1.0 / (lat * n * pix))
+        fin[k, :, 0:width] = xs[0, k, 0:lat, :]
+        fin[k, 0:1, width:] = jnp.sum(jnp.where(diagonal, total, 0.0), axis=0, keepdims=True)
+    each_peer(lambda d: out_copy(d, me).start())
+    final_in[me] = fin[me]
+    each_peer(lambda d: out_copy(d, d).wait_recv())
+    sums = jnp.zeros((1, LANES), f32)
+    for d in range(n):
+        sums = sums + final_in[d, 0:1, width:]
+        if direct:
+            out_ref[0, :, d * pix:(d + 1) * pix] = final_in[d, :, 0:pix]
+        else:
+            out_ref[d] = final_in[d, :, 0:width]
+    means = sums * (1.0 / (copies * lat * n * pix))
     for r in range(ROUNDS):
         err_ref[r] = means[:, r * ITERS:(r + 1) * ITERS]
-    each_peer(lambda d: out_copy(d, d).wait_recv())
     each_peer(lambda d: in_copy(d, me).wait_send())
     each_peer(lambda d: out_copy(d, me).wait_send())
-    each_peer(lambda d: err_copy(d, me).wait_send())
 
 
 def closing(final_ref, errors_ref, final_out, errors_out, sems):
@@ -391,7 +416,7 @@
     depth = round_up(XROWS + 3 * ROUNDS * n, LANES)
     fused = (
         n <= 16 and width == TILE and ch == TILE + LANES // 2 and depth == LANES
-        and (n - ITERS + 1) // 2 > LAG_NOISE and VECTOR_ROWS < ch)
+        and (n - ITERS + 1) // 2 > LAG_NOISE and 0 < VECTOR_ROWS < ch and 2 * lat == 8)
     vector_rows = VECTOR_ROWS if fused else 0
     if direct:
         sent = states
@@ -419,10 +444,9 @@
             pltpu.VMEM((2 * ch, BASE), f32),
             pltpu.VMEM((n, lat, width), f32),
             pltpu.VMEM((ITERS + 1, n, 8, width), f32),
-            pltpu.VMEM((n, lat, width), f32),
+            pltpu.VMEM((n, lat, width + LANES), f32),
+            pltpu.VMEM((n, lat, width + LANES), f32),
             pltpu.VMEM((n, ROUNDS * ITERS, LANES), f32),
-            pltpu.VMEM((n, 1, LANES), f32),
-            pltpu.VMEM((n, 1, LANES), f32),
             pltpu.VMEM((16 + ch - vector_rows, LANES + depth) if fused else (ch, depth), bf16),
             pltpu.VMEM((2, ch + 16, TILE) if fused else (ch, ch), bf16),
             pltpu.VMEM((16, ch), bf16),
@@ -434,8 +458,9 @@
             pltpu.VMEM((ROUNDS * n, max(vector_rows, 8), LANES), f32),
             pltpu.VMEM((lat, 8, LANES), f32),
             pltpu.VMEM((ROUNDS * n, 8, LANES), f32),
+            pltpu.VMEM((ROUNDS * n if fused else 1, depth - XROWS, LANES), bf16),
             pltpu.SemaphoreType.DMA((9,)),
-        ] + [pltpu.SemaphoreType.DMA((n,))] * 6,
+        ] + [pltpu.SemaphoreType.DMA((n,))] * 4,
         compiler_params=pltpu.CompilerParams(
             collective_id=0, has_side_effects=True, vmem_limit_bytes=VMEM_BYTES),
         name="picard",

time: 33.7 us -> 32.1 us (0.953)
  Pallas kernels: 32.9 us -> 31.3 us
    pallas_call x1, Pallas kernels: 32.3 us -> 30.7 us  [shards(): pl.pallas_call(functools.partial(kernel, n, pix, width, depth, direct, ve...]
where the time goes in v3:
time: 32.1 us; the launch traced here: 31.9 us
  Pallas kernels  31.3 us (98%)
  between operations  0.64 us (2%)
    pallas_call x1, Pallas kernels, shards(): pl.pallas_call(functools.partial(kernel, n, pix, width, depth, direct, ve...  30.7 us
    pallas_call x1, Pallas kernels, shards(): pl.pallas_call(closing, out_shape=(pltpu.HBM(out_shape, f32), pltpu.HBM((...  0.65 us

profile of v3, /device:TPU:0, one launch (start us, length us, event | category | flops | bytes accessed | tf_op | source)
XLA Modules:
  0.0 31.9 jit_solution(1882726908286567247)
XLA Ops:
  0.6 30.7 %picard.1 = (f32[1,4,4096]{2,1,0:T(4,128)S(1)}, f32[2,1,4]{2,1,0:T(1,128)S(1)}) custom-call(f32[1,4,4096]{2,1,0:T(4,128)} %states_hbm.1, s32[33]{0:T(128)} %sched_hbm.1, s32[2]{0:T(128)} %adv_hbm.1, f32[1000]{0:T(1024)} %constant.4.clone.alpha_hbm, bf16[4,320]{1,0:T(4,128)(2,1)} %bitcast.4, bf16[4,320]{1,0:T(4,128)(2,1)} %outw_hbm.1, f32[320,320]{1,0:T(8,128)} %timew_hbm.1, ...), custom_call_target="tpu_custom_call" | custom-call | tf_op jit(solution)/shard_map/picard/pallas_call | solution.py:430
  31.3 0.7 %closing.1 = (f32[1,4,4096]{2,1,0:T(4,128)}, f32[2,1,4]{2,1,0:T(1,128)}) custom-call(f32[1,4,4096]{2,1,0:T(4,128)S(1)} %get-tuple-element.6.final_ref, f32[2,1,4]{2,1,0:T(1,128)S(1)} %get-tuple-element.7.errors_ref), custom_call_target="tpu_custom_call" | custom-call | tf_op jit(solution)/shard_map/closing/pallas_call | solution.py:470

commit v4 on v3

--- a/solution.py
+++ b/solution.py
@@ -83,9 +83,9 @@
             src_ref=fin.at[d], dst_ref=final_in.at[slot], send_sem=out_send.at[d], recv_sem=out_recv.at[slot],
             device_id={"steps": d}, device_id_type=pl.DeviceIdType.MESH)
 
-    def each_peer(act):
+    def each_peer(act, near_first=False):
         if n <= 16:
-            for hop in reversed(range(1, n)):
+            for hop in range(1, n) if near_first else reversed(range(1, n)):
                 act(peer(hop))
         else:
             @pl.loop(1, n)
@@ -213,7 +213,7 @@
 
     def place(d, values):
         for copy in range(copies):
-            xs[0, d, copy * lat:(copy + 1) * lat, :] = values
+            xs[ITERS if fused else 0, d, copy * lat:(copy + 1) * lat, :] = values
 
     place(me, states_ref[0, :, pl.ds(pl.multiple_of(me * pix, LANES), pix)] if direct else states_ref[me])
 
@@ -221,7 +221,7 @@
         in_copy(d, d).wait_recv()
         place(d, xin[d])
 
-    each_peer(arrived)
+    each_peer(arrived, near_first=True)
 
     wide = lambda tile: jnp.concatenate([tile] * (width // LANES), axis=1) if width > LANES else tile
 
@@ -263,7 +263,8 @@
         total = square[:, 0:LANES]
         for start in range(LANES, width, LANES):
             total = total + square[:, start:start + LANES]
-        errs[k, pl.ds(row, 1), :] = jnp.sum(total, axis=0, keepdims=True)
+        whole_sum = jnp.sum(jnp.sum(total, axis=0, keepdims=True), axis=1, keepdims=True)
+        errs[k, pl.ds(row, 1), :] = jnp.broadcast_to(whole_sum, (1, LANES))
 
     def moved(r, m_at, old, noise):
         return wide(coef_one[m_at]) * old + wide(coef_two[m_at]) * noise
@@ -357,9 +358,10 @@
     def one_round(r, carry):
         advance = adv_ref[r]
         if fused:
+            behind = jnp.where(r == 0, 0, adv_ref[jnp.maximum(r - 1, 0)])
+            for k in range(n):
+                xs[0, k] = xs[ITERS, jnp.minimum(k + behind, n - 1)]
             flat_round(r)
-            for k in range(n):
-                xs[0, k] = xs[ITERS, jnp.minimum(k + advance, n - 1)]
         else:
             rolled_round(r)
 
@@ -375,12 +377,12 @@
     diagonal = lax.broadcasted_iota(jnp.int32, cells, 0) == lax.broadcasted_iota(jnp.int32, cells, 1)
     fin[...] = jnp.zeros_like(fin)
     for k in range(n):
-        total = jnp.sum(errs[k], axis=1, keepdims=True)
-        fin[k, :, 0:width] = xs[0, k, 0:lat, :]
-        fin[k, 0:1, width:] = jnp.sum(jnp.where(diagonal, total, 0.0), axis=0, keepdims=True)
+        fin[k, :, 0:width] = (
+            xs[ITERS, jnp.minimum(k + adv_ref[ROUNDS - 1], n - 1), 0:lat, :] if fused else xs[0, k, 0:lat, :])
+        fin[k, 0:1, width:] = jnp.sum(jnp.where(diagonal, errs[k], 0.0), axis=0, keepdims=True)
+    final_in[me] = fin[me]
     each_peer(lambda d: out_copy(d, me).start())
-    final_in[me] = fin[me]
-    each_peer(lambda d: out_copy(d, d).wait_recv())
+    each_peer(lambda d: out_copy(d, d).wait_recv(), near_first=True)
     sums = jnp.zeros((1, LANES), f32)
     for d in range(n):
         sums = sums + final_in[d, 0:1, width:]

time: 32.1 us -> 31.9 us (level)
  no operation moved by 1% of the time
where the time goes in v4:
time: 31.9 us; the launch traced here: 31.8 us
  Pallas kernels  31.1 us (97%)
  between operations  0.64 us (2%)
    pallas_call x1, Pallas kernels, shards(): pl.pallas_call(functools.partial(kernel, n, pix, width, depth, direct, ve...  30.5 us
    pallas_call x1, Pallas kernels, shards(): pl.pallas_call(closing, out_shape=(pltpu.HBM(out_shape, f32), pltpu.HBM((...  0.65 us

profile of v4, /device:TPU:0, one launch (start us, length us, event | category | flops | bytes accessed | tf_op | source)
XLA Modules:
  0.0 31.8 jit_solution(14953629590845749435)
XLA Ops:
  0.6 30.5 %picard.1 = (f32[1,4,4096]{2,1,0:T(4,128)S(1)}, f32[2,1,4]{2,1,0:T(1,128)S(1)}) custom-call(f32[1,4,4096]{2,1,0:T(4,128)} %states_hbm.1, s32[33]{0:T(128)} %sched_hbm.1, s32[2]{0:T(128)} %adv_hbm.1, f32[1000]{0:T(1024)} %constant.4.clone.alpha_hbm, bf16[4,320]{1,0:T(4,128)(2,1)} %bitcast.4, bf16[4,320]{1,0:T(4,128)(2,1)} %outw_hbm.1, f32[320,320]{1,0:T(8,128)} %timew_hbm.1, ...), custom_call_target="tpu_custom_call" | custom-call | tf_op jit(solution)/shard_map/picard/pallas_call | solution.py:432
  31.1 0.7 %closing.1 = (f32[1,4,4096]{2,1,0:T(4,128)}, f32[2,1,4]{2,1,0:T(1,128)}) custom-call(f32[1,4,4096]{2,1,0:T(4,128)S(1)} %get-tuple-element.6.final_ref, f32[2,1,4]{2,1,0:T(1,128)S(1)} %get-tuple-element.7.errors_ref), custom_call_target="tpu_custom_call" | custom-call | tf_op jit(solution)/shard_map/closing/pallas_call | solution.py:472

commit v5 on v4

--- a/solution.py
+++ b/solution.py
@@ -222,6 +222,7 @@
         place(d, xin[d])
 
     each_peer(arrived, near_first=True)
+    each_peer(lambda d: in_copy(d, me).wait_send())
 
     wide = lambda tile: jnp.concatenate([tile] * (width // LANES), axis=1) if width > LANES else tile
 
@@ -393,7 +394,6 @@
     means = sums * (1.0 / (copies * lat * n * pix))
     for r in range(ROUNDS):
         err_ref[r] = means[:, r * ITERS:(r + 1) * ITERS]
-    each_peer(lambda d: in_copy(d, me).wait_send())
     each_peer(lambda d: out_copy(d, me).wait_send())
 
 

time: 31.9 us -> 31.9 us (level)
  no operation moved by 1% of the time
where the time goes in v5:
time: 31.9 us; the launch traced here: 31.8 us
  Pallas kernels  31.1 us (97%)
  between operations  0.64 us (2%)
    pallas_call x1, Pallas kernels, shards(): pl.pallas_call(functools.partial(kernel, n, pix, width, depth, direct, ve...  30.5 us
    pallas_call x1, Pallas kernels, shards(): pl.pallas_call(closing, out_shape=(pltpu.HBM(out_shape, f32), pltpu.HBM((...  0.65 us

profile of v5, /device:TPU:0, one launch (start us, length us, event | category | flops | bytes accessed | tf_op | source)
XLA Modules:
  0.0 31.8 jit_solution(4872575079760401789)
XLA Ops:
  0.6 30.5 %picard.1 = (f32[1,4,4096]{2,1,0:T(4,128)S(1)}, f32[2,1,4]{2,1,0:T(1,128)S(1)}) custom-call(f32[1,4,4096]{2,1,0:T(4,128)} %states_hbm.1, s32[33]{0:T(128)} %sched_hbm.1, s32[2]{0:T(128)} %adv_hbm.1, f32[1000]{0:T(1024)} %constant.4.clone.alpha_hbm, bf16[4,320]{1,0:T(4,128)(2,1)} %bitcast.4, bf16[4,320]{1,0:T(4,128)(2,1)} %outw_hbm.1, f32[320,320]{1,0:T(8,128)} %timew_hbm.1, ...), custom_call_target="tpu_custom_call" | custom-call | tf_op jit(solution)/shard_map/picard/pallas_call | solution.py:432
  31.1 0.7 %closing.1 = (f32[1,4,4096]{2,1,0:T(4,128)}, f32[2,1,4]{2,1,0:T(1,128)}) custom-call(f32[1,4,4096]{2,1,0:T(4,128)S(1)} %get-tuple-element.6.final_ref, f32[2,1,4]{2,1,0:T(1,128)S(1)} %get-tuple-element.7.errors_ref), custom_call_target="tpu_custom_call" | custom-call | tf_op jit(solution)/shard_map/closing/pallas_call | solution.py:472
